TPU v7x, 32 devices: a whole 2x2x4 slice. The times are simulated.
32 devices in a mesh: replica: 2 (over y), kv: 4 (over z), head: 2 (over x), sub: 2 (over core).
Axes of the slice: x: 2, y: 2, z: 4, core: 2. Of those that a mesh axis runs over, the one named last changes fastest.
Arguments:
- queries: bfloat16 [256, 64, 128], P(('replica', 'kv'), 'head'), parts along dimension 0, may hold values from -12 to 12
- sys_keys: bfloat16 [16, 1024, 128], P(('replica', 'head'), ('kv', 'sub')), parts along dimension 0, may hold values from -5 to 5
- sys_values: bfloat16 [16, 1024, 128], P(('replica', 'head'), ('kv', 'sub')), parts along dimension 0, may hold values from -6 to 6
- task_keys: bfloat16 [8, 8, 4096, 128], P(('replica', 'kv'), 'head', 'sub'), parts along dimension 0, may hold values from -5 to 5
- task_values: bfloat16 [8, 8, 4096, 128], P(('replica', 'kv'), 'head', 'sub'), parts along dimension 0, may hold values from -6 to 6
- suffix_keys: bfloat16 [256, 8, 512, 128], P(('replica', 'kv', 'sub'), 'head'), parts along dimension 0, may hold values from -5 to 5
- suffix_values: bfloat16 [256, 8, 512, 128], P(('replica', 'kv', 'sub'), 'head'), parts along dimension 0, may hold values from -6 to 6
- task_ids: int32 [256], P(('replica', 'kv')), parts along dimension 0, may hold values from 0 to 3, as said below
- suffix_len: int32 [256], P(('replica', 'kv', 'sub')), parts along dimension 0, may hold values from 256 to 512, as said below
Outputs:
- attended: bfloat16 [256, 64, 128], P(('replica', 'kv', 'sub'), 'head'), parts along dimension 0
There are 2 independent parts, one for each index of `replica`. A program takes and returns all parts, laid end to end along the dimension named above; each array names one. Nothing has to cross between parts.
Inputs may be any that keep to these rules, and one draw needn't show every extreme that they name: `task_ids`: task t's prefix is task_keys[t]. The rows 2 * 16 * p to 2 * 16 * (p + 1) - 1 form aligned blocks; in each block no task is named more than 8 times, and one task, the same for all blocks, is named exactly 8 times in every block. `suffix_len`: each aligned block of 16 rows holds one length equal to 512.
All inputs are finite; a program needn't handle non-finite values.
Results may differ from a plain program's by a relative error of at most 0.005.
Values may be sent and summed in bfloat16 or wider, within the bound.
A program may use at most 64 MiB of HBM per device.

v0:
```python
import functools
import math

import jax
import jax.numpy as jnp
from jax import lax
from jax.experimental import pallas as pl
from jax.experimental.pallas import tpu as pltpu
from jax.sharding import PartitionSpec as P

CAP = 8
NEGATIVE = -1e30
MESH = pl.DeviceIdType.MESH
NT = (((1,), (1,)), ((), ()))
TN = (((0,), (0,)), ((), ()))
F32 = jnp.float32
BF16 = jnp.bfloat16


def dot(a, b, dims=(((1,), (0,)), ((), ()))):
    return lax.dot_general(a, b, dims, preferred_element_type=F32)


def merge(first, second):
    top = jnp.maximum(first[1], second[1])
    a = jnp.exp(first[1] - top)
    b = jnp.exp(second[1] - top)
    total = a + b
    inverse = 1.0 / total
    return first[0] * (a * inverse) + second[0] * (b * inverse), top + jnp.log(total)


def iota(shape, dim):
    return lax.broadcasted_iota(jnp.int32, shape, dim)


def selected(value, picks, pieces):
    out = None
    for _ in range(pieces):
        part = value.astype(BF16)
        value = value - part.astype(F32)
        term = dot(part, picks)
        out = term if out is None else out + term
    return out


def kernel(
    n,
    q_ref,
    sk_ref,
    sv_ref,
    tk_hbm,
    tv_hbm,
    uk_hbm,
    uv_hbm,
    ids_ref,
    len_ref,
    out_ref,
    tk,
    tv,
    uk,
    uv,
    qbuf,
    part_o,
    part_e,
    swap_o,
    swap_e,
    send_o,
    send_e,
    chain_o,
    chain_e,
    fin_o,
    fin_e,
    suf_o,
    suf_e,
    out32,
    task_sem,
    suf_sem,
    own_send,
    z_send,
    z_recv,
    d_send,
    d_recv,
    swap_send,
    swap_recv,
    chain_send,
    chain_recv,
    fin_send,
    fin_recv,
):
    rows, heads, width = q_ref.shape
    kv = sk_ref.shape[0]
    group = heads // kv
    own = uk.shape[0]
    lanes = qbuf.shape[2]
    half = lanes // 2
    task_rows = CAP * group
    scale = 1.0 / math.sqrt(width)
    j = lax.axis_index("kv")
    s = lax.axis_index("sub")
    other = 1 - s

    task_copies = []
    for index, (hbm, buf) in enumerate(((tk_hbm, tk), (tv_hbm, tv))):
        copy = pltpu.make_async_copy(hbm.at[0], buf, task_sem.at[index])
        copy.start()
        task_copies.append(copy)

    def suffix_copies(i):
        return (
            pltpu.make_async_copy(uk_hbm.at[i], uk.at[i], suf_sem.at[0, i]),
            pltpu.make_async_copy(uv_hbm.at[i], uv.at[i], suf_sem.at[1, i]),
        )

    @pl.loop(0, own)
    def _(i):
        for copy in suffix_copies(i):
            copy.start()

    barrier = pltpu.get_barrier_semaphore()
    pl.semaphore_signal(barrier, inc=1, device_id={"sub": other}, device_id_type=MESH)

    @pl.when(j > 0)
    def _():
        pl.semaphore_signal(barrier, inc=1, device_id={"kv": j - 1}, device_id_type=MESH)

    @pl.when(j < n - 1)
    def _():
        pl.semaphore_signal(barrier, inc=1, device_id={"kv": j + 1}, device_id_type=MESH)

    ids = ids_ref[...].astype(F32)
    wide = jnp.broadcast_to(ids, (rows, rows))
    down, across = iota((rows, rows), 0), iota((rows, rows), 1)
    ids_column = jnp.sum(jnp.where(down == across, wide, 0.0), axis=1, keepdims=True)
    same = jnp.where((ids_column == wide) & (down < across), 1.0, 0.0)
    places = ids * CAP + jnp.sum(same, axis=0, keepdims=True)
    places8 = jnp.broadcast_to(places, (8, rows)).astype(BF16)

    def spread(count, base):
        shape = (rows, count * group)
        pick = jnp.where(iota(shape, 0) == base + iota(shape, 1) // group, 1.0, 0.0).astype(BF16)
        row = dot(places8, pick)[0:1].astype(jnp.int32)
        shape = (lanes, count * group)
        down, across = iota(shape, 0), iota(shape, 1)
        hit = (down // group == row) & (down % group == across % group)
        return jnp.where(hit, 1.0, 0.0).astype(BF16)

    everyone = spread(rows, 0)
    wide_query = q_ref[...].astype(F32)
    for k in range(kv):
        mine = wide_query[:, k * group : (k + 1) * group, :].reshape(rows * group, width)
        qbuf[j, k] = dot(everyone, mine.astype(BF16)).astype(BF16)

    pl.semaphore_wait(
        barrier, 1 + jnp.where(j > 0, 1, 0) + jnp.where(j < n - 1, 1, 0)
    )

    def query_view(p, k, h):
        return qbuf.at[p, k, pl.ds(pl.multiple_of(h * half, 16), half), :]

    def query_copy(p, k, send_sem, recv_sem, device):
        return pltpu.make_async_remote_copy(
            src_ref=query_view(p, k, s),
            dst_ref=query_view(p, k, s),
            send_sem=send_sem,
            recv_sem=recv_sem,
            device_id=device,
            device_id_type=MESH,
        )

    def own_copy(k, d):
        return query_copy(j, k, own_send.at[d, k], z_recv.at[j, k], {"kv": j + 2 * d - 1})

    def relay_copy(p, k, d):
        return query_copy(p, k, z_send.at[p, k], z_recv.at[p, k], {"kv": j + 1 - 2 * d})

    def side_copy(p, k):
        return query_copy(p, k, d_send.at[p, k], d_recv.at[p, k], {"sub": other})

    def side_arrival(p, k):
        return pltpu.make_async_remote_copy(
            src_ref=query_view(p, k, other),
            dst_ref=query_view(p, k, other),
            send_sem=d_send.at[p, k],
            recv_sem=d_recv.at[p, k],
            device_id={"sub": other},
            device_id_type=MESH,
        )

    @pl.when(j < n - 1)
    def _():
        for k in range(kv):
            own_copy(k, 1).start()

    @pl.when(j > 0)
    def _():
        for k in range(kv):
            own_copy(k, 0).start()

    def swap_copies(p, k):
        return tuple(
            pltpu.make_async_remote_copy(
                src_ref=src.at[p, other, k],
                dst_ref=dst.at[p, k],
                send_sem=swap_send.at[index, p, k],
                recv_sem=swap_recv.at[index, p, k],
                device_id={"sub": other},
                device_id_type=MESH,
            )
            for index, (src, dst) in enumerate(((part_o, swap_o), (part_e, swap_e)))
        )

    def chain_copies(p, k, d, target=None):
        target = {"kv": j + 2 * d - 1} if target is None else target
        return tuple(
            pltpu.make_async_remote_copy(
                src_ref=src.at[p, k],
                dst_ref=dst.at[d, p, k],
                send_sem=chain_send.at[index, p, k],
                recv_sem=chain_recv.at[index, d, p, k],
                device_id=target,
                device_id_type=MESH,
            )
            for index, (src, dst) in enumerate(((send_o, chain_o), (send_e, chain_e)))
        )

    def fin_copies(k):
        return tuple(
            pltpu.make_async_remote_copy(
                src_ref=buf.at[s, k],
                dst_ref=buf.at[s, k],
                send_sem=fin_send.at[index, k],
                recv_sem=fin_recv.at[index, k],
                device_id={"sub": other},
                device_id_type=MESH,
            )
            for index, buf in enumerate((fin_o, fin_e))
        )

    def fin_arrivals(k):
        return tuple(
            pltpu.make_async_remote_copy(
                src_ref=buf.at[other, k],
                dst_ref=buf.at[other, k],
                send_sem=fin_send.at[index, k],
                recv_sem=fin_recv.at[index, k],
                device_id={"sub": other},
                device_id_type=MESH,
            )
            for index, buf in enumerate((fin_o, fin_e))
        )

    def attend(keys, values, query):
        scores = dot(keys, query, NT)
        maxima = jnp.max(scores, axis=0, keepdims=True)
        weights = jnp.exp((scores - maxima) * scale)
        totals = jnp.sum(weights, axis=0, keepdims=True)
        return maxima * scale, totals, dot(values, weights.astype(BF16), TN)

    def block(p, d):
        def arrive(k):
            @pl.when(jnp.logical_not(beyond(d)))
            def _():
                relay_copy(p, k, d).wait_recv()
                side_copy(p, k).start()

        for k in range(kv):
            if d is not None:
                for later in ([0, 1] if k == 0 else [k + 1]):
                    if later < kv:
                        arrive(later)
                side_arrival(p, k).wait_recv()
            top, total, numerator = attend(sk_ref[k], sv_ref[k], qbuf[p, k])
            system = (numerator * (1.0 / total), top + jnp.log(total))
            picked = qbuf[p, k, pl.ds(pl.multiple_of(j * task_rows, 16), task_rows), :]
            doubled = jnp.concatenate([picked, picked], axis=0)
            tokens = tk.shape[1]
            step = min(512, tokens)
            state = None
            for base in range(0, tokens, step):
                part = attend(
                    tk[k, base : base + step, :], tv[k, base : base + step, :], doubled
                )
                if state is None:
                    state = part
                else:
                    top = jnp.maximum(state[0], part[0])
                    a, b = jnp.exp(state[0] - top), jnp.exp(part[0] - top)
                    state = (top, state[1] * a + part[1] * b, state[2] * a + part[2] * b)
            top, total, numerator = state
            repeats = lanes // (2 * task_rows)
            place = iota((1, lanes), 1) // task_rows == j
            task = (
                jnp.concatenate([numerator * (1.0 / total)] * repeats, axis=1),
                jnp.where(
                    place, jnp.concatenate([top + jnp.log(total)] * repeats, axis=1), NEGATIVE
                ),
            )
            result, level = merge(system, task)
            for h in range(2):
                part_o[p, h, k] = result[:, h * half : (h + 1) * half]
                part_e[p, h, k] = jnp.broadcast_to(level[:, h * half : (h + 1) * half], (8, half))
            for copy in swap_copies(p, k):
                copy.start()

    def chip_part(p, k):
        return merge(
            (part_o[p, s, k], part_e[p, s, k][0:1]), (swap_o[p, k], swap_e[p, k][0:1])
        )

    def chain_part(d, p, k):
        return chain_o[d, p, k].astype(F32), chain_e[d, p, k][0:1]

    def finish(p, d, incoming):
        for k in range(kv):
            for copy in swap_copies(p, k):
                copy.wait_recv()
            state = chip_part(p, k)
            if incoming:
                for copy in chain_copies(p, k, d):
                    copy.wait_recv()
                state = merge(state, chain_part(d, p, k))
            send_o[p, k] = state[0].astype(BF16)
            send_e[p, k] = jnp.broadcast_to(state[1], (8, half))
            for copy in chain_copies(p, k, d):
                copy.start()

    def suffix(i):
        for copy in suffix_copies(i):
            copy.wait()
        query = q_ref[s * own + i].astype(F32)
        length = len_ref[i]
        scores = jnp.concatenate(
            [
                dot(query[k * group : (k + 1) * group].astype(BF16), uk[i, k], NT)
                for k in range(kv)
            ],
            axis=0,
        )
        usable = iota(scores.shape, 1) < length
        scores = jnp.where(usable, scores, NEGATIVE)
        maxima = jnp.max(scores, axis=1, keepdims=True)
        weights = jnp.where(usable, jnp.exp((scores - maxima) * scale), 0.0)
        totals = jnp.sum(weights, axis=1, keepdims=True)
        numerator = jnp.concatenate(
            [
                dot(weights[k * group : (k + 1) * group].astype(BF16), uv[i, k])
                for k in range(kv)
            ],
            axis=0,
        )
        suf_o[i] = numerator * (1.0 / totals)
        suf_e[i] = jnp.broadcast_to(maxima * scale + jnp.log(totals), (heads, width))

    def source(t, d):
        return j + (2 * d - 1) * t

    def valid(t, d):
        p = source(t, d)
        return (p >= 0) & (p < n)

    def beyond(d):
        return jnp.where(d == 0, j < n - 1, j > 0)

    early = own // 4
    late, turns = own - early, 2 * n - 2

    @pl.loop(0, early)
    def _(i):
        suffix(i)

    for copy in task_copies:
        copy.wait()

    @pl.loop(1, n)
    def _(t):
        for k in range(kv):
            for d in range(2):

                @pl.when(valid(t, d) & beyond(d))
                def _(d=d, k=k):
                    p = source(t, d)
                    relay_copy(p, k, d).wait_recv()
                    relay_copy(p, k, d).start()
                    side_copy(p, k).start()

        @pl.loop(0, 2)
        def _(d):
            @pl.when(valid(t, d))
            def _():
                block(source(t, d), d)

        for d in range(2):

            @pl.when(valid(t, d) & jnp.logical_not(beyond(d)))
            def _(d=d):
                finish(source(t, d), d, False)

    block(j, None)

    @pl.loop(1, 2 * n - 1)
    def _(turn):
        @pl.loop(early + (turn - 1) * late // turns, early + turn * late // turns)
        def _(i):
            suffix(i)

        low = 2 * (n - 1) - j - turn

        @pl.when((low >= 0) & (low < j) & (j < n - 1))
        def _():
            finish(low, 0, True)

        high = turn - j

        @pl.when((high > j) & (high < n) & (j > 0))
        def _():
            finish(high, 1, True)

    for k in range(kv):
        for copy in swap_copies(j, k):
            copy.wait_recv()
        value, level = chip_part(j, k)
        fin_o[s, k] = value
        fin_e[s, k] = jnp.broadcast_to(level, (8, half))
    chosen = spread(own, s * own)
    for k in range(kv):
        for d in range(2):

            @pl.when(j < n - 1 if d == 0 else j > 0)
            def _(d=d, k=k):
                for copy in chain_copies(j, k, d, {"kv": j + 1 - 2 * d}):
                    copy.wait_recv()
                state = merge((fin_o[s, k], fin_e[s, k][0:1]), chain_part(d, j, k))
                fin_o[s, k] = state[0]
                fin_e[s, k] = jnp.broadcast_to(state[1], (8, half))

        for copy in fin_copies(k):
            copy.start()
    for k in range(kv):
        for copy in fin_arrivals(k):
            copy.wait_recv()
        value = jnp.concatenate([fin_o[0, k], fin_o[1, k]], axis=1)
        level = jnp.concatenate([fin_e[0, k], fin_e[1, k]], axis=1)
        value = selected(value, chosen, 2).T
        level = jnp.broadcast_to(selected(level, chosen, 3)[0:1], (width, own * group)).T
        near = slice(k * group, (k + 1) * group)
        suffix_state = (
            suf_o[:, near, :].reshape(own * group, width),
            suf_e[:, near, :].reshape(own * group, width),
        )
        attended = merge((value, level), suffix_state)[0]
        out32[:, near, :] = attended.reshape(own, group, width)
    out_ref[...] = out32[...].astype(BF16)

    for k in range(kv):

        @pl.when(j < n - 1)
        def _(k=k):
            own_copy(k, 1).wait_send()

        @pl.when(j > 0)
        def _(k=k):
            own_copy(k, 0).wait_send()

        for copy in swap_copies(j, k) + fin_copies(k):
            copy.wait_send()

    @pl.loop(1, n)
    def _(t):
        for d in range(2):

            @pl.when(valid(t, d))
            def _(d=d):
                p = source(t, d)
                for k in range(kv):

                    @pl.when(beyond(d))
                    def _(k=k):
                        relay_copy(p, k, d).wait_send()

                    side_copy(p, k).wait_send()
                    for copy in swap_copies(p, k) + chain_copies(p, k, d):
                        copy.wait_send()


def body(
    queries,
    sys_keys,
    sys_values,
    task_keys,
    task_values,
    suffix_keys,
    suffix_values,
    task_ids,
    suffix_len,
):
    n = lax.axis_size("kv")
    rows, heads, width = queries.shape
    kv = sys_keys.shape[0]
    group = heads // kv
    own = suffix_keys.shape[0]
    lanes = n * CAP * group
    half = lanes // 2
    vmem = pl.BlockSpec(memory_space=pltpu.VMEM)
    anywhere = pl.BlockSpec(memory_space=pl.ANY)
    dma = pltpu.SemaphoreType.DMA
    return pl.pallas_call(
        functools.partial(kernel, n),
        out_shape=jax.ShapeDtypeStruct((own, heads, width), BF16),
        in_specs=[vmem] * 3 + [anywhere] * 4 + [vmem, pl.BlockSpec(memory_space=pltpu.SMEM)],
        out_specs=vmem,
        scratch_shapes=[
            pltpu.VMEM(task_keys.shape[1:], BF16),
            pltpu.VMEM(task_values.shape[1:], BF16),
            pltpu.VMEM(suffix_keys.shape, BF16),
            pltpu.VMEM(suffix_values.shape, BF16),
            pltpu.VMEM((n, kv, lanes, width), BF16),
            pltpu.VMEM((n, 2, kv, width, half), F32),
            pltpu.VMEM((n, 2, kv, 8, half), F32),
            pltpu.VMEM((n, kv, width, half), F32),
            pltpu.VMEM((n, kv, 8, half), F32),
            pltpu.VMEM((n, kv, width, half), BF16),
            pltpu.VMEM((n, kv, 8, half), F32),
            pltpu.VMEM((2, n, kv, width, half), BF16),
            pltpu.VMEM((2, n, kv, 8, half), F32),
            pltpu.VMEM((2, kv, width, half), F32),
            pltpu.VMEM((2, kv, 8, half), F32),
            pltpu.VMEM((own, heads, width), F32),
            pltpu.VMEM((own, heads, width), F32),
            pltpu.VMEM((own, heads, width), F32),
            dma((2,)),
            dma((2, own)),
            dma((2, kv)),
            dma((n, kv)),
            dma((n, kv)),
            dma((n, kv)),
            dma((n, kv)),
            dma((2, n, kv)),
            dma((2, n, kv)),
            dma((2, n, kv)),
            dma((2, 2, n, kv)),
            dma((2, kv)),
            dma((2, kv)),
        ],
        compiler_params=pltpu.CompilerParams(
            collective_id=0, has_side_effects=True, vmem_limit_bytes=60 * 1024 * 1024
        ),
        name="cascade",
    )(
        queries,
        sys_keys,
        sys_values,
        task_keys,
        task_values,
        suffix_keys,
        suffix_values,
        task_ids.reshape(1, rows),
        suffix_len,
    )


def solution(mesh):
    in_specs = (
        P(("replica", "kv"), "head", None),
        P(("replica", "head"), ("kv", "sub"), None),
        P(("replica", "head"), ("kv", "sub"), None),
        P(("replica", "kv"), "head", "sub", None),
        P(("replica", "kv"), "head", "sub", None),
        P(("replica", "kv", "sub"), "head", None, None),
        P(("replica", "kv", "sub"), "head", None, None),
        P(("replica", "kv")),
        P(("replica", "kv", "sub")),
    )
    out_specs = P(("replica", "kv", "sub"), "head", None)
    return jax.shard_map(body, mesh=mesh, in_specs=in_specs, out_specs=out_specs, check_vma=False)
```

profile of v0, /device:TPU:0, one launch (start us, length us, event | category | flops | bytes accessed | tf_op | source)
XLA Modules:
  0.0 44.2 jit_solution(4144531673290121887)
XLA Ops:
  0.0 42.7 %cascade.1 = bf16[16,32,128]{2,1,0:T(8,128)(2,1)} custom-call(bf16[32,32,128]{2,1,0:T(8,128)(2,1)} %q_ref.1, bf16[4,128,128]{2,1,0:T(8,128)(2,1)} %sk_ref.1, bf16[4,128,128]{2,1,0:T(8,128)(2,1)} %sv_ref.1, bf16[1,4,2048,128]{3,2,1,0:T(8,128)(2,1)} %tk_hbm.1, bf16[1,4,2048,128]{3,2,1,0:T(8,128)(2,1)} %tv_hbm.1, bf16[16,4,512,128]{3,2,1,0:T(8,128)(2,1)} %uk_hbm.1, ...), custom_call_target="tpu_custom_call" | custom-call | tf_op jit(solution)/shard_map/cascade/pallas_call | solution.py:507
  42.7 1.6 %copy.11 = bf16[16,32,128]{2,1,0:T(8,128)(2,1)} copy(bf16[16,32,128]{2,1,0:T(8,128)(2,1)} %cascade.1) | data formatting | bytes 262144
where the time goes:
time: 44.4 us; the launch traced here: 44.2 us
  Pallas kernels  42.7 us (96%)
  local copies, waits for them, and re-layouts  1.57 us (4%)
    pallas_call x1, Pallas kernels, body(): pl.pallas_call(functools.partial(kernel, n), out_shape=jax.ShapeDtypeStru...  42.7 us
    unnamed x1, local copies, waits for them, and re-layouts  1.57 us

commit v1 on v0

--- a/solution.py
+++ b/solution.py
@@ -483,6 +483,622 @@
                         copy.wait_send()
 
 
+def exp2(x):
+    return jnp.exp2(x)
+
+
+def blend(parts):
+    top = parts[0][1]
+    for part in parts[1:]:
+        top = jnp.maximum(top, part[1])
+    factors = [exp2(part[1] - top) for part in parts]
+    total = sum(factors[1:], factors[0])
+    inverse = 1.0 / total
+    value = parts[0][0] * (factors[0] * inverse)
+    for part, factor in zip(parts[1:], factors[1:]):
+        value = value + part[0] * (factor * inverse)
+    return value, top + jnp.log2(total)
+
+
+def paired(
+    n,
+    q_hbm,
+    sk_hbm,
+    sv_hbm,
+    tk_hbm,
+    tv_hbm,
+    uk_hbm,
+    uv_hbm,
+    ids_hbm,
+    len_hbm,
+    out_hbm,
+    qh,
+    qo,
+    ids_ref,
+    len_ref,
+    perm,
+    qs,
+    tq,
+    qx,
+    sysb,
+    taskb,
+    uk,
+    uv,
+    suf_o,
+    suf_e,
+    sib_o,
+    sib_e,
+    base_o,
+    base_e,
+    rs_o,
+    rs_e,
+    rr_o,
+    rr_e,
+    ps_o,
+    ps_e,
+    pr_o,
+    pr_e,
+    out32,
+    outb,
+    load_sem,
+    sysl_sem,
+    task_sem,
+    suf_sem,
+    tx_send,
+    tx_recv,
+    sys_send,
+    sys_recv,
+    q_send,
+    q_recv,
+    ret_send,
+    ret_recv,
+    sx_send,
+    sx_recv,
+    fin_sem,
+    fin_send,
+    fin_recv,
+):
+    rows = qh.shape[0]
+    own, heads, width = qo.shape
+    mine = qh.shape[1]
+    kv = uk.shape[1]
+    group = heads // kv
+    per = kv // 2
+    half_n = n // 2
+    cell = CAP * group
+    lanes = 2 * half_n * cell
+    tile = 2 * cell
+    shard = sk_hbm.shape[1]
+    stretch = tk_hbm.shape[2]
+    scale = math.log2(math.e) / math.sqrt(width)
+    j = lax.axis_index("kv")
+    s = lax.axis_index("sub")
+    other = 1 - s
+    side = j // half_n
+    e = j % half_n
+    mate = j + 1 - 2 * e
+    far = (1 - side) * half_n
+
+    barrier = pltpu.get_barrier_semaphore()
+    pl.semaphore_signal(barrier, inc=1, device_id={"sub": other}, device_id_type=MESH)
+    for d in range(1, n):
+        target = lax.rem(j + d, n)
+        for z in range(2):
+            pl.semaphore_signal(
+                barrier, inc=1, device_id={"kv": target, "sub": z}, device_id_type=MESH
+            )
+
+    def remote(src, dst, send_sem, recv_sem, device):
+        return pltpu.make_async_remote_copy(
+            src_ref=src,
+            dst_ref=dst,
+            send_sem=send_sem,
+            recv_sem=recv_sem,
+            device_id=device,
+            device_id_type=MESH,
+        )
+
+    first = pl.multiple_of(s * mine, 16)
+    loads = [
+        pltpu.make_async_copy(ids_hbm, ids_ref, load_sem.at[0]),
+        pltpu.make_async_copy(q_hbm.at[:, pl.ds(first, mine), :], qh, load_sem.at[1]),
+        pltpu.make_async_copy(q_hbm.at[pl.ds(s * own, own)], qo, load_sem.at[2]),
+        pltpu.make_async_copy(len_hbm, len_ref, load_sem.at[3]),
+    ]
+    for copy in loads:
+        copy.start()
+
+    def spot(chip, core):
+        return pl.ds(pl.multiple_of((2 * chip + core) * shard, 128), shard)
+
+    sys_local = [
+        pltpu.make_async_copy(
+            hbm.at[pl.ds(s * per, per)], sysb.at[kind, :, spot(e, s), :], sysl_sem.at[kind]
+        )
+        for kind, hbm in enumerate((sk_hbm, sv_hbm))
+    ]
+    for copy in sys_local:
+        copy.start()
+
+    def strip(core):
+        return pl.ds(pl.multiple_of(core * stretch, 128), stretch)
+
+    task_local = [
+        [
+            pltpu.make_async_copy(
+                hbm.at[0, s * per + h], taskb.at[kind, h, strip(s), :], task_sem.at[kind, h]
+            )
+            for kind, hbm in enumerate((tk_hbm, tv_hbm))
+        ]
+        for h in range(per)
+    ]
+    for copies in task_local:
+        for copy in copies:
+            copy.start()
+
+    def suffix_copies(i):
+        return (
+            pltpu.make_async_copy(uk_hbm.at[i], uk.at[i], suf_sem.at[0, i]),
+            pltpu.make_async_copy(uv_hbm.at[i], uv.at[i], suf_sem.at[1, i]),
+        )
+
+    @pl.loop(0, own)
+    def _(i):
+        for copy in suffix_copies(i):
+            copy.start()
+
+    loads[0].wait()
+    ids = ids_ref[...]
+    names = ids.astype(F32)
+    wide = jnp.broadcast_to(names, (rows, rows))
+    down, across = iota((rows, rows), 0), iota((rows, rows), 1)
+    column = jnp.sum(jnp.where(down == across, wide, 0.0), axis=1, keepdims=True)
+    same = jnp.where((column == wide) & (down < across), 1.0, 0.0)
+    seat = ids % half_n
+    seat = jnp.where(ids // half_n == side, half_n - 1 - seat, half_n + seat)
+    places = seat.astype(F32) * CAP + jnp.sum(same, axis=0, keepdims=True)
+    places8 = jnp.broadcast_to(places, (8, rows)).astype(BF16)
+    shape = (rows, rows * group)
+    pick = jnp.where(iota(shape, 0) == iota(shape, 1) // group, 1.0, 0.0).astype(BF16)
+    row = dot(places8, pick)[0:1].astype(jnp.int32)
+    shape = (lanes, rows * group)
+    down, across = iota(shape, 0), iota(shape, 1)
+    hit = (down // group == row) & (down % group == across % group)
+    perm[...] = jnp.where(hit, 1.0, 0.0).astype(BF16)
+    loads[1].wait()
+    wide_query = qh[...].astype(F32)
+    for h in range(per):
+        flat = wide_query[:, h * group : (h + 1) * group, :].reshape(rows * group, width)
+        qs[h] = dot(perm[...], flat.astype(BF16)).astype(BF16)
+
+    def cellat(base):
+        return pl.ds(pl.multiple_of(base, 16), cell)
+
+    for h in range(per):
+        tq[h, cellat((1 - e) * cell), :] = qs[h, cellat((1 - e) * cell), :]
+
+    def query_copies(h):
+        copies = [
+            remote(
+                qs.at[h, cellat(e * cell), :],
+                tq.at[h, cellat(tile + e * cell), :],
+                q_send.at[h, 0],
+                q_recv.at[h, 0],
+                {"kv": mate},
+            )
+        ]
+        for c in range(2):
+            copies.append(
+                remote(
+                    qs.at[h, cellat(tile + c * cell), :],
+                    tq.at[h, cellat(e * tile + c * cell), :],
+                    q_send.at[h, 1 + c],
+                    q_recv.at[h, 1 + e],
+                    {"kv": far + c},
+                )
+            )
+            copies.append(
+                remote(
+                    qs.at[h, cellat((1 - c) * cell), :],
+                    qx.at[h, cellat(e * tile + (1 - c) * cell), :],
+                    q_send.at[h, 3 + c],
+                    q_recv.at[h, 3 + e],
+                    {"kv": far + c},
+                )
+            )
+        return copies
+
+    def query_arrivals(h):
+        places = [(tq, tile + (1 - e) * cell)]
+        places += [(tq, i * tile + e * cell) for i in range(2)]
+        places += [(qx, i * tile + (1 - e) * cell) for i in range(2)]
+        return [
+            remote(
+                buf.at[h, cellat(base), :],
+                buf.at[h, cellat(base), :],
+                q_send.at[h, index],
+                q_recv.at[h, index],
+                {"kv": mate},
+            )
+            for index, (buf, base) in enumerate(places)
+        ]
+
+    def sys_copies(h):
+        copies = []
+        for kind, hbm in enumerate((sk_hbm, sv_hbm)):
+            dst = sysb.at[kind, h, spot(e, s), :]
+            copies.append(
+                remote(
+                    hbm.at[other * per + h],
+                    dst,
+                    sys_send.at[kind, h, 0],
+                    sys_recv.at[kind, h, 0],
+                    {"sub": other},
+                )
+            )
+            for z in range(2):
+                copies.append(
+                    remote(
+                        hbm.at[z * per + h],
+                        dst,
+                        sys_send.at[kind, h, 1 + z],
+                        sys_recv.at[kind, h, 1 + s],
+                        {"kv": mate, "sub": z},
+                    )
+                )
+        return copies
+
+    def sys_arrivals(h):
+        out = []
+        for kind in range(2):
+            for index, (chip, core) in enumerate(((e, other), (1 - e, 0), (1 - e, 1))):
+                ref = sysb.at[kind, h, spot(chip, core), :]
+                out.append(
+                    remote(
+                        ref,
+                        ref,
+                        sys_send.at[kind, h, index],
+                        sys_recv.at[kind, h, index],
+                        {"sub": other},
+                    )
+                )
+        return out
+
+    def task_copies(h):
+        return [
+            remote(
+                hbm.at[0, other * per + h],
+                taskb.at[kind, h, strip(s), :],
+                tx_send.at[kind, h],
+                tx_recv.at[kind, h],
+                {"sub": other},
+            )
+            for kind, hbm in enumerate((tk_hbm, tv_hbm))
+        ]
+
+    def task_arrivals(h):
+        return [
+            remote(
+                taskb.at[kind, h, strip(other), :],
+                taskb.at[kind, h, strip(other), :],
+                tx_send.at[kind, h],
+                tx_recv.at[kind, h],
+                {"sub": other},
+            )
+            for kind in range(2)
+        ]
+
+    pl.semaphore_wait(barrier, 2 * n - 1)
+    for h in range(per):
+        for copy in query_copies(h) + sys_copies(h) + task_copies(h):
+            copy.start()
+
+    def suffix(i):
+        for copy in suffix_copies(i):
+            copy.wait()
+        query = qo[i].astype(F32)
+        length = len_ref[i]
+        scores = jnp.concatenate(
+            [
+                dot(query[k * group : (k + 1) * group].astype(BF16), uk[i, k], NT)
+                for k in range(kv)
+            ],
+            axis=0,
+        )
+        usable = iota(scores.shape, 1) < length
+        scores = jnp.where(usable, scores, NEGATIVE)
+        maxima = jnp.max(scores, axis=1, keepdims=True)
+        weights = jnp.where(usable, exp2((scores - maxima) * scale), 0.0)
+        totals = jnp.sum(weights, axis=1, keepdims=True)
+        numerator = jnp.concatenate(
+            [
+                dot(weights[k * group : (k + 1) * group].astype(BF16), uv[i, k])
+                for k in range(kv)
+            ],
+            axis=0,
+        )
+        value = numerator * (1.0 / totals)
+        level = jnp.broadcast_to(maxima * scale + jnp.log2(totals), (heads, width))
+        for z in range(2):
+            suf_o[z, i] = value[z * mine : (z + 1) * mine]
+            suf_e[z, i] = level[z * mine : (z + 1) * mine]
+
+    def sweep(pairs, query):
+        state = None
+        scores = dot(pairs[0][0](), query, NT)
+        for index, (_, values) in enumerate(pairs):
+            later = dot(pairs[index + 1][0](), query, NT) if index + 1 < len(pairs) else None
+            top = jnp.max(scores, axis=0, keepdims=True)
+            weights = exp2((scores - top) * scale)
+            total = jnp.sum(weights, axis=0, keepdims=True)
+            part = (top * scale, total, dot(values(), weights.astype(BF16), TN))
+            if state is None:
+                state = part
+            else:
+                top = jnp.maximum(state[0], part[0])
+                a, b = exp2(state[0] - top), exp2(part[0] - top)
+                state = (top, state[1] * a + part[1] * b, state[2] * a + part[2] * b)
+            scores = later
+        top, total, numerator = state
+        return numerator * (1.0 / total), top + jnp.log2(total)
+
+    def pieces(buf, h, step):
+        tokens = buf.shape[2]
+        step = min(step, tokens)
+        return [
+            (
+                lambda base=base: buf[0, h, base : base + step, :],
+                lambda base=base: buf[1, h, base : base + step, :],
+            )
+            for base in range(0, tokens, step)
+        ]
+
+    zone = iota((1, tile), 1) // cell
+
+    def ret_copies(h, i):
+        return [
+            remote(
+                src.at[h, i],
+                dst.at[h, e],
+                ret_send.at[index, h, i],
+                ret_recv.at[index, h, e],
+                {"kv": far + i},
+            )
+            for index, (src, dst) in enumerate(((rs_o, rr_o), (rs_e, rr_e)))
+        ]
+
+    def ret_arrivals(h, i):
+        return [
+            remote(
+                dst.at[h, i],
+                dst.at[h, i],
+                ret_send.at[index, h, i],
+                ret_recv.at[index, h, i],
+                {"kv": far + i},
+            )
+            for index, dst in enumerate((rr_o, rr_e))
+        ]
+
+    def mate_copies(h):
+        return [
+            remote(
+                src.at[h],
+                dst.at[h],
+                ret_send.at[index, h, 2],
+                ret_recv.at[index, h, 2],
+                {"kv": mate},
+            )
+            for index, (src, dst) in enumerate(((ps_o, pr_o), (ps_e, pr_e)))
+        ]
+
+    def head(h):
+        for copy in task_local[h] + ([] if h else sys_local):
+            copy.wait()
+        for copy in query_arrivals(h) + task_arrivals(h):
+            copy.wait_recv()
+        for i in range(2):
+            qx[h, cellat(i * tile + e * cell), :] = tq[h, cellat(i * tile + e * cell), :]
+        value, level = sweep(pieces(taskb, h, 512), tq[h])
+        near = value[:, tile:]
+        packed = jnp.where(
+            zone == 1 - e,
+            near[: width // 2],
+            pltpu.roll(near[width // 2 :], cell, 1),
+        )
+        ps_o[h] = packed.astype(BF16)
+        ps_e[h] = jnp.broadcast_to(level[:, tile:], (8, tile))
+        for copy in mate_copies(h):
+            copy.start()
+        for copy in sys_arrivals(h):
+            copy.wait_recv()
+        cross, cross_level = sweep(pieces(sysb, h, 512), qx[h])
+        for i in range(2):
+            cut = slice(i * tile, (i + 1) * tile)
+            task_level = jnp.where(zone == e, level[:, cut], NEGATIVE)
+            merged = blend([(cross[:, cut], cross_level[:, cut]), (value[:, cut], task_level)])
+            rs_o[h, i] = merged[0].astype(BF16)
+            rs_e[h, i] = jnp.broadcast_to(merged[1], (8, tile))
+            for copy in ret_copies(h, i):
+                copy.start()
+        home, home_level = sweep(pieces(sysb, h, 512), qs[h])
+        task_level = jnp.where(zone == 1 - e, level[:, :tile], NEGATIVE)
+        merged = blend([(home[:, :tile], home_level[:, :tile]), (value[:, :tile], task_level)])
+        base_o[h] = jnp.concatenate([merged[0], home[:, tile:]], axis=1)
+        base_e[h] = jnp.broadcast_to(
+            jnp.concatenate([merged[1], home_level[:, tile:]], axis=1), (8, lanes)
+        )
+
+    def exchange():
+        return [
+            remote(
+                src.at[other],
+                dst,
+                sx_send.at[index],
+                sx_recv.at[index],
+                {"sub": other},
+            )
+            for index, (src, dst) in enumerate(((suf_o, sib_o), (suf_e, sib_e)))
+        ]
+
+    def span(core):
+        return pl.ds(pl.multiple_of(core * own * group, 128), own * group)
+
+    def fold(h):
+        value, level = None, None
+        for core, o_ref, e_ref in ((s, suf_o.at[s], suf_e.at[s]), (other, sib_o, sib_e)):
+            near = slice(h * group, (h + 1) * group)
+            rest = o_ref[:, near, :].reshape(own * group, width)
+            tall = e_ref[:, near, :].reshape(own * group, width)
+            chosen = perm[:, span(core)]
+            for _ in range(2):
+                piece = rest.astype(BF16)
+                rest = rest - piece.astype(F32)
+                term = dot(piece, chosen, (((0,), (1,)), ((), ())))
+                value = term if value is None else value + term
+            tall = tall.T[0:1]
+            term = jnp.sum(jnp.where(chosen.astype(F32) > 0.5, tall, 0.0), axis=1, keepdims=True)
+            level = term if level is None else level + term
+        level = jnp.broadcast_to(level, (lanes, width)).T[0:1]
+        merged = blend([(base_o[h], base_e[h][0:1]), (value, level)])
+        base_o[h] = merged[0]
+        base_e[h] = jnp.broadcast_to(merged[1], (8, lanes))
+
+    def finish(h):
+        for copy in ret_arrivals(h, 0) + ret_arrivals(h, 1) + mate_copies(h):
+            copy.wait_recv()
+        low = zone == 0
+        far_o = [rr_o[h, c].astype(F32) for c in range(2)]
+        far_e = [rr_e[h, c][0:1] for c in range(2)]
+        crossed = [
+            (jnp.where(low, far_o[1], far_o[0]), jnp.where(low, far_e[1], far_e[0])),
+            (jnp.where(low, far_o[0], far_o[1]), jnp.where(low, far_e[0], far_e[1])),
+        ]
+        packed = pr_o[h].astype(F32)
+        near = jnp.concatenate([packed, pltpu.roll(packed, cell, 1)], axis=0)
+        near_level = jnp.where(zone == e, pr_e[h][0:1], NEGATIVE)
+        results = []
+        for i in range(2):
+            cut = slice(i * tile, (i + 1) * tile)
+            parts = [(base_o[h, :, cut], base_e[h, 0:1, cut]), crossed[i]]
+            if i == 0:
+                parts.append((near, near_level))
+            results.append(blend(parts)[0])
+        done = jnp.concatenate(results, axis=1).astype(BF16)
+        for index, core in enumerate((other, s)):
+            chosen = perm[:, span(core)]
+            ordered = dot(chosen, done, (((0,), (1,)), ((), ())))
+            out32[index, :, h * group : (h + 1) * group, :] = ordered.reshape(own, group, width)
+
+    for copy in loads[2:]:
+        copy.wait()
+    early = own
+    @pl.loop(0, early)
+    def _(i):
+        suffix(i)
+
+    for copy in exchange():
+        copy.start()
+    for h in range(per):
+        head(h)
+    for copy in exchange():
+        copy.wait_recv()
+    for h in range(per):
+        fold(h)
+    for h in range(per):
+        finish(h)
+    outb[0] = out32[0].astype(BF16)
+    mine_cut = out_hbm.at[:, pl.ds(first, mine), :]
+    give = remote(outb.at[0], mine_cut, fin_send, fin_recv, {"sub": other})
+    give.start()
+    outb[1] = out32[1].astype(BF16)
+    keep = pltpu.make_async_copy(outb.at[1], mine_cut, fin_sem)
+    keep.start()
+
+    for h in range(per):
+        for copy in query_copies(h) + sys_copies(h) + task_copies(h):
+            copy.wait_send()
+        for copy in mate_copies(h) + ret_copies(h, 0) + ret_copies(h, 1):
+            copy.wait_send()
+    for copy in exchange():
+        copy.wait_send()
+    keep.wait()
+    give.wait_send()
+    theirs = out_hbm.at[:, pl.ds(pl.multiple_of(other * mine, 16), mine), :]
+    remote(outb.at[0], theirs, fin_send, fin_recv, {"sub": other}).wait_recv()
+
+
+def paired_call(n, args, out_shape):
+    queries, sys_keys, _, task_keys, _, suffix_keys, _, task_ids, _ = args
+    rows, heads, width = queries.shape
+    kv = sys_keys.shape[0]
+    group = heads // kv
+    own = suffix_keys.shape[0]
+    per = kv // 2
+    mine = heads // 2
+    cell = CAP * group
+    tile = 2 * cell
+    lanes = n * cell
+    anywhere = pl.BlockSpec(memory_space=pl.ANY)
+    dma = pltpu.SemaphoreType.DMA
+    return pl.pallas_call(
+        functools.partial(paired, n),
+        out_shape=out_shape,
+        in_specs=[anywhere] * 9,
+        out_specs=anywhere,
+        scratch_shapes=[
+            pltpu.VMEM((rows, mine, width), BF16),
+            pltpu.VMEM((own, heads, width), BF16),
+            pltpu.VMEM((1, rows), jnp.int32),
+            pltpu.SMEM((own,), jnp.int32),
+            pltpu.VMEM((lanes, rows * group), BF16),
+            pltpu.VMEM((per, lanes, width), BF16),
+            pltpu.VMEM((per, lanes, width), BF16),
+            pltpu.VMEM((per, lanes, width), BF16),
+            pltpu.VMEM((2, per, n * sys_keys.shape[1], width), BF16),
+            pltpu.VMEM((2, per, 2 * task_keys.shape[2], width), BF16),
+            pltpu.VMEM(suffix_keys.shape, BF16),
+            pltpu.VMEM(suffix_keys.shape, BF16),
+            pltpu.VMEM((2, own, mine, width), F32),
+            pltpu.VMEM((2, own, mine, width), F32),
+            pltpu.VMEM((own, mine, width), F32),
+            pltpu.VMEM((own, mine, width), F32),
+            pltpu.VMEM((per, width, lanes), F32),
+            pltpu.VMEM((per, 8, lanes), F32),
+            pltpu.VMEM((per, 2, width, tile), BF16),
+            pltpu.VMEM((per, 2, 8, tile), F32),
+            pltpu.VMEM((per, 2, width, tile), BF16),
+            pltpu.VMEM((per, 2, 8, tile), F32),
+            pltpu.VMEM((per, width // 2, tile), BF16),
+            pltpu.VMEM((per, 8, tile), F32),
+            pltpu.VMEM((per, width // 2, tile), BF16),
+            pltpu.VMEM((per, 8, tile), F32),
+            pltpu.VMEM((2, own, mine, width), F32),
+            pltpu.VMEM((2, own, mine, width), BF16),
+            dma((4,)),
+            dma((2,)),
+            dma((2, per)),
+            dma((2, own)),
+            dma((2, per)),
+            dma((2, per)),
+            dma((2, per, 3)),
+            dma((2, per, 3)),
+            dma((per, 5)),
+            dma((per, 5)),
+            dma((2, per, 3)),
+            dma((2, per, 3)),
+            dma((2,)),
+            dma((2,)),
+            dma,
+            dma,
+            dma,
+        ],
+        compiler_params=pltpu.CompilerParams(
+            collective_id=0, has_side_effects=True, vmem_limit_bytes=60 * 1024 * 1024
+        ),
+        name="cascade",
+    )(*args[:7], task_ids.reshape(1, rows), args[8])
+
+
 def body(
     queries,
     sys_keys,
@@ -501,12 +1117,26 @@
     own = suffix_keys.shape[0]
     lanes = n * CAP * group
     half = lanes // 2
+    out_shape = jax.ShapeDtypeStruct((own, heads, width), BF16)
+    if n == 4 and rows == n * CAP and kv % 2 == 0 and 2 * CAP * group == width:
+        args = (
+            queries,
+            sys_keys,
+            sys_values,
+            task_keys,
+            task_values,
+            suffix_keys,
+            suffix_values,
+            task_ids,
+            suffix_len,
+        )
+        return paired_call(n, args, out_shape)
     vmem = pl.BlockSpec(memory_space=pltpu.VMEM)
     anywhere = pl.BlockSpec(memory_space=pl.ANY)
     dma = pltpu.SemaphoreType.DMA
     return pl.pallas_call(
         functools.partial(kernel, n),
-        out_shape=jax.ShapeDtypeStruct((own, heads, width), BF16),
+        out_shape=out_shape,
         in_specs=[vmem] * 3 + [anywhere] * 4 + [vmem, pl.BlockSpec(memory_space=pltpu.SMEM)],
         out_specs=vmem,
         scratch_shapes=[

time: 44.4 us -> 27.1 us (0.61)
  Pallas kernels: 42.7 us -> 25.4 us
    pallas_call x1, Pallas kernels: 42.7 us -> 25.4 us  [paired_call(): pl.pallas_call(functools.partial(paired, n), out_shape=out_shape, in_spec...]
where the time goes in v1:
time: 27.1 us; the launch traced here: 27 us
  Pallas kernels  25.4 us (94%)
  local copies, waits for them, and re-layouts  1.57 us (6%)
    pallas_call x1, Pallas kernels, paired_call(): pl.pallas_call(functools.partial(paired, n), out_shape=out_shape, in_spec...  25.4 us
    unnamed x1, local copies, waits for them, and re-layouts  1.57 us

profile of v1, /device:TPU:0, one launch (start us, length us, event | category | flops | bytes accessed | tf_op | source)
XLA Modules:
  0.0 27.0 jit_solution(11751443710894587838)
XLA Ops:
  0.0 25.4 %cascade.1 = bf16[16,32,128]{2,1,0:T(8,128)(2,1)} custom-call(bf16[32,32,128]{2,1,0:T(8,128)(2,1)} %q_hbm.1, bf16[4,128,128]{2,1,0:T(8,128)(2,1)} %sk_hbm.1, bf16[4,128,128]{2,1,0:T(8,128)(2,1)} %sv_hbm.1, bf16[1,4,2048,128]{3,2,1,0:T(8,128)(2,1)} %tk_hbm.1, bf16[1,4,2048,128]{3,2,1,0:T(8,128)(2,1)} %tv_hbm.1, bf16[16,4,512,128]{3,2,1,0:T(8,128)(2,1)} %uk_hbm.1, ...), custom_call_target="tpu_custom_call" | custom-call | tf_op jit(solution)/shard_map/cascade/pallas_call | solution.py:1043
  25.4 1.6 %copy.11 = bf16[16,32,128]{2,1,0:T(8,128)(2,1)} copy(bf16[16,32,128]{2,1,0:T(8,128)(2,1)} %cascade.1) | data formatting | bytes 262144

commit v2 on v1

--- a/solution.py
+++ b/solution.py
@@ -483,8 +483,8 @@
                         copy.wait_send()
 
 
-def exp2(x):
-    return jnp.exp2(x)
+exp2 = jnp.exp2
+scope = jax.named_scope
 
 
 def blend(parts):
@@ -632,22 +632,26 @@
         ]
         for h in range(per)
     ]
-    for copies in task_local:
-        for copy in copies:
-            copy.start()
-
     def suffix_copies(i):
         return (
             pltpu.make_async_copy(uk_hbm.at[i], uk.at[i], suf_sem.at[0, i]),
             pltpu.make_async_copy(uv_hbm.at[i], uv.at[i], suf_sem.at[1, i]),
         )
 
-    @pl.loop(0, own)
-    def _(i):
-        for copy in suffix_copies(i):
+    def fetch(low, high):
+        @pl.loop(low, high)
+        def _(i):
+            for copy in suffix_copies(i):
+                copy.start()
+
+    fetch(0, own // 4)
+    for copies in task_local:
+        for copy in copies:
             copy.start()
-
-    loads[0].wait()
+    fetch(own // 4, own)
+
+    with scope("ids"):
+        loads[0].wait()
     ids = ids_ref[...]
     names = ids.astype(F32)
     wide = jnp.broadcast_to(names, (rows, rows))
@@ -788,78 +792,94 @@
             for kind in range(2)
         ]
 
-    pl.semaphore_wait(barrier, 2 * n - 1)
-    for h in range(per):
-        for copy in query_copies(h) + sys_copies(h) + task_copies(h):
-            copy.start()
-
-    def suffix(i):
-        for copy in suffix_copies(i):
-            copy.wait()
-        query = qo[i].astype(F32)
-        length = len_ref[i]
-        scores = jnp.concatenate(
-            [
-                dot(query[k * group : (k + 1) * group].astype(BF16), uk[i, k], NT)
-                for k in range(kv)
-            ],
-            axis=0,
-        )
-        usable = iota(scores.shape, 1) < length
-        scores = jnp.where(usable, scores, NEGATIVE)
-        maxima = jnp.max(scores, axis=1, keepdims=True)
-        weights = jnp.where(usable, exp2((scores - maxima) * scale), 0.0)
-        totals = jnp.sum(weights, axis=1, keepdims=True)
-        numerator = jnp.concatenate(
-            [
-                dot(weights[k * group : (k + 1) * group].astype(BF16), uv[i, k])
-                for k in range(kv)
-            ],
-            axis=0,
-        )
-        value = numerator * (1.0 / totals)
-        level = jnp.broadcast_to(maxima * scale + jnp.log2(totals), (heads, width))
-        for z in range(2):
-            suf_o[z, i] = value[z * mine : (z + 1) * mine]
-            suf_e[z, i] = level[z * mine : (z + 1) * mine]
-
-    def sweep(pairs, query):
-        state = None
-        scores = dot(pairs[0][0](), query, NT)
-        for index, (_, values) in enumerate(pairs):
-            later = dot(pairs[index + 1][0](), query, NT) if index + 1 < len(pairs) else None
+    def suffix(base):
+        picks = range(4)
+        for r in picks:
+            for copy in suffix_copies(base + r):
+                copy.wait()
+        scores = []
+        for r in picks:
+            query = qo[base + r].astype(F32)
+            scores.append(
+                jnp.concatenate(
+                    [
+                        dot(
+                            query[k * group : (k + 1) * group].astype(BF16),
+                            uk[base + r, k],
+                            NT,
+                        )
+                        for k in range(kv)
+                    ],
+                    axis=0,
+                )
+            )
+        states = []
+        for r in picks:
+            usable = iota(scores[r].shape, 1) < len_ref[base + r]
+            masked = jnp.where(usable, scores[r], NEGATIVE)
+            maxima = jnp.max(masked, axis=1, keepdims=True)
+            weights = jnp.where(usable, exp2((masked - maxima) * scale), 0.0)
+            states.append((maxima, weights, jnp.sum(weights, axis=1, keepdims=True)))
+        for r in picks:
+            maxima, weights, totals = states[r]
+            numerator = jnp.concatenate(
+                [
+                    dot(weights[k * group : (k + 1) * group].astype(BF16), uv[base + r, k])
+                    for k in range(kv)
+                ],
+                axis=0,
+            )
+            value = numerator * (1.0 / totals)
+            level = jnp.broadcast_to(maxima * scale + jnp.log2(totals), (heads, width))
+            for z in range(2):
+                suf_o[z, base + r] = value[z * mine : (z + 1) * mine]
+                suf_e[z, base + r] = level[z * mine : (z + 1) * mine]
+
+    def sweep(items):
+        states = {}
+        ahead = [dot(item[1](), item[3], NT) for item in items[:1]]
+        for index, (name, _, values, _) in enumerate(items):
+            scores = ahead.pop(0)
+            if index + 1 < len(items):
+                item = items[index + 1]
+                ahead.append(dot(item[1](), item[3], NT))
             top = jnp.max(scores, axis=0, keepdims=True)
             weights = exp2((scores - top) * scale)
             total = jnp.sum(weights, axis=0, keepdims=True)
             part = (top * scale, total, dot(values(), weights.astype(BF16), TN))
-            if state is None:
-                state = part
-            else:
+            if name in states:
+                state = states[name]
                 top = jnp.maximum(state[0], part[0])
                 a, b = exp2(state[0] - top), exp2(part[0] - top)
-                state = (top, state[1] * a + part[1] * b, state[2] * a + part[2] * b)
-            scores = later
-        top, total, numerator = state
-        return numerator * (1.0 / total), top + jnp.log2(total)
-
-    def pieces(buf, h, step):
+                part = (top, state[1] * a + part[1] * b, state[2] * a + part[2] * b)
+            states[name] = part
+        return {
+            name: (numerator * (1.0 / total), top + jnp.log2(total))
+            for name, (top, total, numerator) in states.items()
+        }
+
+    def pieces(name, buf, h, step, query):
         tokens = buf.shape[2]
         step = min(step, tokens)
         return [
             (
+                name,
                 lambda base=base: buf[0, h, base : base + step, :],
                 lambda base=base: buf[1, h, base : base + step, :],
+                query,
             )
             for base in range(0, tokens, step)
         ]
 
     zone = iota((1, tile), 1) // cell
+
+    slim = (slice(None), pl.ds(0, 1))
 
     def ret_copies(h, i):
         return [
             remote(
-                src.at[h, i],
-                dst.at[h, e],
+                src.at[h, i, slim[index]],
+                dst.at[h, e, slim[index]],
                 ret_send.at[index, h, i],
                 ret_recv.at[index, h, e],
                 {"kv": far + i},
@@ -870,8 +890,8 @@
     def ret_arrivals(h, i):
         return [
             remote(
-                dst.at[h, i],
-                dst.at[h, i],
+                dst.at[h, i, slim[index]],
+                dst.at[h, i, slim[index]],
                 ret_send.at[index, h, i],
                 ret_recv.at[index, h, i],
                 {"kv": far + i},
@@ -882,8 +902,8 @@
     def mate_copies(h):
         return [
             remote(
-                src.at[h],
-                dst.at[h],
+                src.at[h, slim[index]],
+                dst.at[h, slim[index]],
                 ret_send.at[index, h, 2],
                 ret_recv.at[index, h, 2],
                 {"kv": mate},
@@ -891,14 +911,39 @@
             for index, (src, dst) in enumerate(((ps_o, pr_o), (ps_e, pr_e)))
         ]
 
-    def head(h):
-        for copy in task_local[h] + ([] if h else sys_local):
-            copy.wait()
-        for copy in query_arrivals(h) + task_arrivals(h):
-            copy.wait_recv()
+    def arrive(h):
+        with scope("local"):
+            for copy in task_local[h]:
+                copy.wait()
+        with scope("queries"):
+            for copy in query_arrivals(h):
+                copy.wait_recv()
+        with scope("taskwait"):
+            for copy in task_arrivals(h):
+                copy.wait_recv()
+
+    def system(h):
+        with scope("syswait"):
+            if h == 0:
+                for copy in sys_local:
+                    copy.wait()
+            for copy in sys_arrivals(h):
+                copy.wait_recv()
+
+    def gather(h):
         for i in range(2):
             qx[h, cellat(i * tile + e * cell), :] = tq[h, cellat(i * tile + e * cell), :]
-        value, level = sweep(pieces(taskb, h, 512), tq[h])
+
+    def task_items(h):
+        return pieces("task", taskb, h, 1024, tq[h])
+
+    def cross_items(h):
+        return pieces("cross", sysb, h, 1024, qx[h])
+
+    def keep_task(h, found):
+        value, level = found
+        base_o[h] = value
+        base_e[h] = jnp.broadcast_to(level, (8, lanes))
         near = value[:, tile:]
         packed = jnp.where(
             zone == 1 - e,
@@ -907,26 +952,29 @@
         )
         ps_o[h] = packed.astype(BF16)
         ps_e[h] = jnp.broadcast_to(level[:, tile:], (8, tile))
-        for copy in mate_copies(h):
-            copy.start()
-        for copy in sys_arrivals(h):
-            copy.wait_recv()
-        cross, cross_level = sweep(pieces(sysb, h, 512), qx[h])
+
+    def keep_cross(h, found, task):
+        value, level = found
         for i in range(2):
             cut = slice(i * tile, (i + 1) * tile)
-            task_level = jnp.where(zone == e, level[:, cut], NEGATIVE)
-            merged = blend([(cross[:, cut], cross_level[:, cut]), (value[:, cut], task_level)])
+            task_level = jnp.where(zone == e, task[1][:, cut], NEGATIVE)
+            merged = blend([(value[:, cut], level[:, cut]), (task[0][:, cut], task_level)])
             rs_o[h, i] = merged[0].astype(BF16)
             rs_e[h, i] = jnp.broadcast_to(merged[1], (8, tile))
-            for copy in ret_copies(h, i):
-                copy.start()
-        home, home_level = sweep(pieces(sysb, h, 512), qs[h])
-        task_level = jnp.where(zone == 1 - e, level[:, :tile], NEGATIVE)
-        merged = blend([(home[:, :tile], home_level[:, :tile]), (value[:, :tile], task_level)])
-        base_o[h] = jnp.concatenate([merged[0], home[:, tile:]], axis=1)
-        base_e[h] = jnp.broadcast_to(
-            jnp.concatenate([merged[1], home_level[:, tile:]], axis=1), (8, lanes)
-        )
+
+    def home():
+        items = []
+        for h in range(per):
+            items += pieces(h, sysb, h, 1024, qs[h])
+        found = sweep(items)
+        for h in range(per):
+            value, level = found[h]
+            task_level = jnp.where(zone == 1 - e, base_e[h, 0:1, :tile], NEGATIVE)
+            merged = blend([(value[:, :tile], level[:, :tile]), (base_o[h, :, :tile], task_level)])
+            base_o[h] = jnp.concatenate([merged[0], value[:, tile:]], axis=1)
+            base_e[h] = jnp.broadcast_to(
+                jnp.concatenate([merged[1], level[:, tile:]], axis=1), (8, lanes)
+            )
 
     def exchange():
         return [
@@ -964,8 +1012,9 @@
         base_e[h] = jnp.broadcast_to(merged[1], (8, lanes))
 
     def finish(h):
-        for copy in ret_arrivals(h, 0) + ret_arrivals(h, 1) + mate_copies(h):
-            copy.wait_recv()
+        with scope("retwait"):
+            for copy in ret_arrivals(h, 0) + ret_arrivals(h, 1) + mate_copies(h):
+                copy.wait_recv()
         low = zone == 0
         far_o = [rr_o[h, c].astype(F32) for c in range(2)]
         far_e = [rr_e[h, c][0:1] for c in range(2)]
@@ -991,21 +1040,61 @@
 
     for copy in loads[2:]:
         copy.wait()
-    early = own
-    @pl.loop(0, early)
-    def _(i):
-        suffix(i)
-
+
+    def suffixes(low, high):
+        with scope("suffix"):
+
+            @pl.loop(low, high)
+            def _(i):
+                suffix(i * 4)
+
+    ahead = (3 * own * (n - 1 - j)) // (32 * n)
+    suffixes(0, ahead)
+    with scope("barrier"):
+        pl.semaphore_wait(barrier, 2 * n - 1)
+    for copy in query_copies(0) + sys_copies(0) + task_copies(0):
+        copy.start()
+    suffixes(ahead, 2)
+    with scope("drain"):
+        for copy in query_copies(0):
+            copy.wait_send()
+    for copy in query_copies(1) + sys_copies(1) + task_copies(1):
+        copy.start()
+    suffixes(2, own // 4)
     for copy in exchange():
         copy.start()
+    arrive(0)
+    system(0)
+    with scope("block"):
+        gather(0)
+        found = sweep(task_items(0) + cross_items(0))
+        keep_cross(0, found["cross"], found["task"])
+        keep_task(0, found["task"])
+        for copy in ret_copies(0, 0) + ret_copies(0, 1) + mate_copies(0):
+            copy.start()
+    arrive(1)
+    with scope("task"):
+        gather(1)
+        keep_task(1, sweep(task_items(1))["task"])
+        for copy in mate_copies(1):
+            copy.start()
+    system(1)
+    with scope("cross"):
+        task = (base_o[1], base_e[1, 0:1])
+        keep_cross(1, sweep(cross_items(1))["cross"], task)
+        for copy in ret_copies(1, 0) + ret_copies(1, 1):
+            copy.start()
+    with scope("home"):
+        home()
+    with scope("sxwait"):
+        for copy in exchange():
+            copy.wait_recv()
+    with scope("fold"):
+        for h in range(per):
+            fold(h)
     for h in range(per):
-        head(h)
-    for copy in exchange():
-        copy.wait_recv()
-    for h in range(per):
-        fold(h)
-    for h in range(per):
-        finish(h)
+        with scope("finish"):
+            finish(h)
     outb[0] = out32[0].astype(BF16)
     mine_cut = out_hbm.at[:, pl.ds(first, mine), :]
     give = remote(outb.at[0], mine_cut, fin_send, fin_recv, {"sub": other})
@@ -1014,17 +1103,18 @@
     keep = pltpu.make_async_copy(outb.at[1], mine_cut, fin_sem)
     keep.start()
 
+    for copy in sys_copies(0) + task_copies(0) + query_copies(1) + sys_copies(1) + task_copies(1):
+        copy.wait_send()
     for h in range(per):
-        for copy in query_copies(h) + sys_copies(h) + task_copies(h):
-            copy.wait_send()
         for copy in mate_copies(h) + ret_copies(h, 0) + ret_copies(h, 1):
             copy.wait_send()
     for copy in exchange():
         copy.wait_send()
-    keep.wait()
-    give.wait_send()
-    theirs = out_hbm.at[:, pl.ds(pl.multiple_of(other * mine, 16), mine), :]
-    remote(outb.at[0], theirs, fin_send, fin_recv, {"sub": other}).wait_recv()
+    with scope("tail"):
+        keep.wait()
+        give.wait_send()
+        theirs = out_hbm.at[:, pl.ds(pl.multiple_of(other * mine, 16), mine), :]
+        remote(outb.at[0], theirs, fin_send, fin_recv, {"sub": other}).wait_recv()
 
 
 def paired_call(n, args, out_shape):
@@ -1038,13 +1128,12 @@
     cell = CAP * group
     tile = 2 * cell
     lanes = n * cell
-    anywhere = pl.BlockSpec(memory_space=pl.ANY)
     dma = pltpu.SemaphoreType.DMA
     return pl.pallas_call(
         functools.partial(paired, n),
         out_shape=out_shape,
-        in_specs=[anywhere] * 9,
-        out_specs=anywhere,
+        in_specs=[pl.BlockSpec(memory_space=pl.ANY)] * 9,
+        out_specs=pl.BlockSpec(memory_space=pl.ANY),
         scratch_shapes=[
             pltpu.VMEM((rows, mine, width), BF16),
             pltpu.VMEM((own, heads, width), BF16),

time: 27.1 us -> 25.3 us (0.934)
  Pallas kernels: 25.4 us -> 23.6 us
    pallas_call x1, Pallas kernels: 25.4 us -> 23.6 us  [paired_call(): pl.pallas_call(functools.partial(paired, n), out_shape=out_shape, in_spec...]
where the time goes in v2:
time: 25.3 us; the launch traced here: 25.1 us
  Pallas kernels  23.6 us (93%)
  local copies, waits for them, and re-layouts  1.57 us (6%)
    pallas_call x1, Pallas kernels, paired_call(): pl.pallas_call(functools.partial(paired, n), out_shape=out_shape, in_spec...  23.6 us
    unnamed x1, local copies, waits for them, and re-layouts  1.57 us

profile of v2, /device:TPU:0, one launch (start us, length us, event | category | flops | bytes accessed | tf_op | source)
XLA Modules:
  0.0 25.1 jit_solution(13585984046329570783)
XLA Ops:
  0.0 23.6 %cascade.1 = bf16[16,32,128]{2,1,0:T(8,128)(2,1)} custom-call(bf16[32,32,128]{2,1,0:T(8,128)(2,1)} %q_hbm.1, bf16[4,128,128]{2,1,0:T(8,128)(2,1)} %sk_hbm.1, bf16[4,128,128]{2,1,0:T(8,128)(2,1)} %sv_hbm.1, bf16[1,4,2048,128]{3,2,1,0:T(8,128)(2,1)} %tk_hbm.1, bf16[1,4,2048,128]{3,2,1,0:T(8,128)(2,1)} %tv_hbm.1, bf16[16,4,512,128]{3,2,1,0:T(8,128)(2,1)} %uk_hbm.1, ...), custom_call_target="tpu_custom_call" | custom-call | tf_op jit(solution)/shard_map/cascade/pallas_call | solution.py:1132
  23.6 1.6 %copy.11 = bf16[16,32,128]{2,1,0:T(8,128)(2,1)} copy(bf16[16,32,128]{2,1,0:T(8,128)(2,1)} %cascade.1) | data formatting | bytes 262144

commit v3 on v2

--- a/solution.py
+++ b/solution.py
@@ -511,7 +511,7 @@
     uv_hbm,
     ids_hbm,
     len_hbm,
-    out_hbm,
+    out_ref,
     qh,
     qo,
     ids_ref,
@@ -554,7 +554,6 @@
     ret_recv,
     sx_send,
     sx_recv,
-    fin_sem,
     fin_send,
     fin_recv,
 ):
@@ -1054,15 +1053,16 @@
         pl.semaphore_wait(barrier, 2 * n - 1)
     for copy in query_copies(0) + sys_copies(0) + task_copies(0):
         copy.start()
-    suffixes(ahead, 2)
+    suffixes(ahead, 1)
+    for copy in query_copies(1):
+        copy.start()
+    suffixes(1, 2)
     with scope("drain"):
         for copy in query_copies(0):
             copy.wait_send()
-    for copy in query_copies(1) + sys_copies(1) + task_copies(1):
+    for copy in sys_copies(1) + task_copies(1):
         copy.start()
-    suffixes(2, own // 4)
-    for copy in exchange():
-        copy.start()
+    suffixes(2, own // 4 - 1)
     arrive(0)
     system(0)
     with scope("block"):
@@ -1084,6 +1084,9 @@
         keep_cross(1, sweep(cross_items(1))["cross"], task)
         for copy in ret_copies(1, 0) + ret_copies(1, 1):
             copy.start()
+    suffixes(own // 4 - 1, own // 4)
+    for copy in exchange():
+        copy.start()
     with scope("home"):
         home()
     with scope("sxwait"):
@@ -1095,13 +1098,10 @@
     for h in range(per):
         with scope("finish"):
             finish(h)
-    outb[0] = out32[0].astype(BF16)
-    mine_cut = out_hbm.at[:, pl.ds(first, mine), :]
-    give = remote(outb.at[0], mine_cut, fin_send, fin_recv, {"sub": other})
+    outb[...] = out32[0].astype(BF16)
+    give = remote(outb, out_ref.at[:, pl.ds(first, mine), :], fin_send, fin_recv, {"sub": other})
     give.start()
-    outb[1] = out32[1].astype(BF16)
-    keep = pltpu.make_async_copy(outb.at[1], mine_cut, fin_sem)
-    keep.start()
+    out_ref[:, pl.ds(first, mine), :] = out32[1].astype(BF16)
 
     for copy in sys_copies(0) + task_copies(0) + query_copies(1) + sys_copies(1) + task_copies(1):
         copy.wait_send()
@@ -1111,10 +1111,9 @@
     for copy in exchange():
         copy.wait_send()
     with scope("tail"):
-        keep.wait()
         give.wait_send()
-        theirs = out_hbm.at[:, pl.ds(pl.multiple_of(other * mine, 16), mine), :]
-        remote(outb.at[0], theirs, fin_send, fin_recv, {"sub": other}).wait_recv()
+        theirs = out_ref.at[:, pl.ds(pl.multiple_of(other * mine, 16), mine), :]
+        remote(outb, theirs, fin_send, fin_recv, {"sub": other}).wait_recv()
 
 
 def paired_call(n, args, out_shape):
@@ -1129,11 +1128,12 @@
     tile = 2 * cell
     lanes = n * cell
     dma = pltpu.SemaphoreType.DMA
+    inputs = (*args[:7], task_ids.reshape(1, rows), args[8])
     return pl.pallas_call(
         functools.partial(paired, n),
         out_shape=out_shape,
         in_specs=[pl.BlockSpec(memory_space=pl.ANY)] * 9,
-        out_specs=pl.BlockSpec(memory_space=pl.ANY),
+        out_specs=pl.BlockSpec(memory_space=pltpu.VMEM),
         scratch_shapes=[
             pltpu.VMEM((rows, mine, width), BF16),
             pltpu.VMEM((own, heads, width), BF16),
@@ -1162,7 +1162,7 @@
             pltpu.VMEM((per, width // 2, tile), BF16),
             pltpu.VMEM((per, 8, tile), F32),
             pltpu.VMEM((2, own, mine, width), F32),
-            pltpu.VMEM((2, own, mine, width), BF16),
+            pltpu.VMEM((own, mine, width), BF16),
             dma((4,)),
             dma((2,)),
             dma((2, per)),
@@ -1179,13 +1179,12 @@
             dma((2,)),
             dma,
             dma,
-            dma,
         ],
         compiler_params=pltpu.CompilerParams(
-            collective_id=0, has_side_effects=True, vmem_limit_bytes=60 * 1024 * 1024
+            collective_id=0, has_side_effects=True, vmem_limit_bytes=48 * 1024 * 1024
         ),
         name="cascade",
-    )(*args[:7], task_ids.reshape(1, rows), args[8])
+    )(*(pltpu.with_memory_space_constraint(x, pltpu.HBM) for x in inputs))
 
 
 def body(

time: 25.3 us -> 24.2 us (0.957)
  local copies, waits for them, and re-layouts: 1.57 us -> 0.66 us
    unnamed x1, local copies, waits for them, and re-layouts: 1.57 us -> 0.66 us
where the time goes in v3:
time: 24.2 us; the launch traced here: 24.1 us
  Pallas kernels  23.4 us (97%)
  local copies, waits for them, and re-layouts  0.66 us (3%)
    pallas_call x1, Pallas kernels, paired_call(): pl.pallas_call(functools.partial(paired, n), out_shape=out_shape, in_spec...  23.4 us
    unnamed x1, local copies, waits for them, and re-layouts  0.66 us

profile of v3, /device:TPU:0, one launch (start us, length us, event | category | flops | bytes accessed | tf_op | source)
XLA Modules:
  0.0 24.1 jit_solution(15626976797852113016)
XLA Ops:
  0.0 23.4 %cascade.1 = bf16[16,32,128]{2,1,0:T(8,128)(2,1)S(1)} custom-call(bf16[32,32,128]{2,1,0:T(8,128)(2,1)} %q_hbm.1, bf16[4,128,128]{2,1,0:T(8,128)(2,1)} %sk_hbm.1, bf16[4,128,128]{2,1,0:T(8,128)(2,1)} %sv_hbm.1, bf16[1,4,2048,128]{3,2,1,0:T(8,128)(2,1)} %tk_hbm.1, bf16[1,4,2048,128]{3,2,1,0:T(8,128)(2,1)} %tv_hbm.1, bf16[16,4,512,128]{3,2,1,0:T(8,128)(2,1)} %uk_hbm.1, ...), custom_call_target="tpu_custom_call" | custom-call | tf_op jit(solution)/shard_map/cascade/pallas_call | solution.py:1132
  23.4 0.7 %copy.11 = bf16[16,32,128]{2,1,0:T(8,128)(2,1)} copy(bf16[16,32,128]{2,1,0:T(8,128)(2,1)S(1)} %cascade.1) | data formatting | bytes 262144

commit v4 on v3

--- a/solution.py
+++ b/solution.py
@@ -1051,15 +1051,33 @@
     suffixes(0, ahead)
     with scope("barrier"):
         pl.semaphore_wait(barrier, 2 * n - 1)
-    for copy in query_copies(0) + sys_copies(0) + task_copies(0):
+    rank = e + side
+
+    @pl.when(rank != 9)
+    def _():
+        for copy in query_copies(0):
+            copy.start()
+
+    @pl.when(rank == 0)
+    def _():
+        for copy in query_copies(1):
+            copy.start()
+
+    for copy in sys_copies(0) + task_copies(0):
         copy.start()
-    suffixes(ahead, 1)
-    for copy in query_copies(1):
-        copy.start()
-    suffixes(1, 2)
-    with scope("drain"):
+
+    @pl.when(rank == 9)
+    def _():
         for copy in query_copies(0):
-            copy.wait_send()
+            copy.start()
+
+    suffixes(ahead, 2)
+    @pl.when(rank != 0)
+    def _():
+        for copy in query_copies(1):
+            copy.start()
+
+    suffixes(2, 2)
     for copy in sys_copies(1) + task_copies(1):
         copy.start()
     suffixes(2, own // 4 - 1)
@@ -1103,7 +1121,7 @@
     give.start()
     out_ref[:, pl.ds(first, mine), :] = out32[1].astype(BF16)
 
-    for copy in sys_copies(0) + task_copies(0) + query_copies(1) + sys_copies(1) + task_copies(1):
+    for copy in query_copies(0) + sys_copies(0) + task_copies(0) + query_copies(1) + sys_copies(1) + task_copies(1):
         copy.wait_send()
     for h in range(per):
         for copy in mate_copies(h) + ret_copies(h, 0) + ret_copies(h, 1):

time: 24.2 us -> 23.3 us (0.963)
  Pallas kernels: 23.4 us -> 22.5 us
    pallas_call x1, Pallas kernels: 23.4 us -> 22.5 us  [paired_call(): pl.pallas_call(functools.partial(paired, n), out_shape=out_shape, in_spec...]
where the time goes in v4:
time: 23.3 us; the launch traced here: 23.2 us
  Pallas kernels  22.5 us (97%)
  local copies, waits for them, and re-layouts  0.66 us (3%)
    pallas_call x1, Pallas kernels, paired_call(): pl.pallas_call(functools.partial(paired, n), out_shape=out_shape, in_spec...  22.5 us
    unnamed x1, local copies, waits for them, and re-layouts  0.66 us

profile of v4, /device:TPU:0, one launch (start us, length us, event | category | flops | bytes accessed | tf_op | source)
XLA Modules:
  0.0 23.2 jit_solution(12313981459575618389)
XLA Ops:
  0.0 22.5 %cascade.1 = bf16[16,32,128]{2,1,0:T(8,128)(2,1)S(1)} custom-call(bf16[32,32,128]{2,1,0:T(8,128)(2,1)} %q_hbm.1, bf16[4,128,128]{2,1,0:T(8,128)(2,1)} %sk_hbm.1, bf16[4,128,128]{2,1,0:T(8,128)(2,1)} %sv_hbm.1, bf16[1,4,2048,128]{3,2,1,0:T(8,128)(2,1)} %tk_hbm.1, bf16[1,4,2048,128]{3,2,1,0:T(8,128)(2,1)} %tv_hbm.1, bf16[16,4,512,128]{3,2,1,0:T(8,128)(2,1)} %uk_hbm.1, ...), custom_call_target="tpu_custom_call" | custom-call | tf_op jit(solution)/shard_map/cascade/pallas_call | solution.py:1150
  22.5 0.7 %copy.11 = bf16[16,32,128]{2,1,0:T(8,128)(2,1)} copy(bf16[16,32,128]{2,1,0:T(8,128)(2,1)S(1)} %cascade.1) | data formatting | bytes 262144

commit v5 on v4

--- a/solution.py
+++ b/solution.py
@@ -1047,8 +1047,6 @@
             def _(i):
                 suffix(i * 4)
 
-    ahead = (3 * own * (n - 1 - j)) // (32 * n)
-    suffixes(0, ahead)
     with scope("barrier"):
         pl.semaphore_wait(barrier, 2 * n - 1)
     rank = e + side
@@ -1071,7 +1069,7 @@
         for copy in query_copies(0):
             copy.start()
 
-    suffixes(ahead, 2)
+    suffixes(0, 2)
     @pl.when(rank != 0)
     def _():
         for copy in query_copies(1):

time: 23.3 us -> 23.3 us (level)
  no operation moved by 1% of the time
where the time goes in v5:
time: 23.3 us; the launch traced here: 23.2 us
  Pallas kernels  22.5 us (97%)
  local copies, waits for them, and re-layouts  0.66 us (3%)
    pallas_call x1, Pallas kernels, paired_call(): pl.pallas_call(functools.partial(paired, n), out_shape=out_shape, in_spec...  22.5 us
    unnamed x1, local copies, waits for them, and re-layouts  0.66 us

profile of v5, /device:TPU:0, one launch (start us, length us, event | category | flops | bytes accessed | tf_op | source)
XLA Modules:
  0.0 23.2 jit_solution(9210453781239360045)
XLA Ops:
  0.0 22.5 %cascade.1 = bf16[16,32,128]{2,1,0:T(8,128)(2,1)S(1)} custom-call(bf16[32,32,128]{2,1,0:T(8,128)(2,1)} %q_hbm.1, bf16[4,128,128]{2,1,0:T(8,128)(2,1)} %sk_hbm.1, bf16[4,128,128]{2,1,0:T(8,128)(2,1)} %sv_hbm.1, bf16[1,4,2048,128]{3,2,1,0:T(8,128)(2,1)} %tk_hbm.1, bf16[1,4,2048,128]{3,2,1,0:T(8,128)(2,1)} %tv_hbm.1, bf16[16,4,512,128]{3,2,1,0:T(8,128)(2,1)} %uk_hbm.1, ...), custom_call_target="tpu_custom_call" | custom-call | tf_op jit(solution)/shard_map/cascade/pallas_call | solution.py:1148
  22.5 0.7 %copy.11 = bf16[16,32,128]{2,1,0:T(8,128)(2,1)} copy(bf16[16,32,128]{2,1,0:T(8,128)(2,1)S(1)} %cascade.1) | data formatting | bytes 262144
